TPU v7x, 256 devices: a 2x2x32 block of a 4x8x32 slice. The times are simulated.
256 devices in a mesh: groups: 4 (over x, y), expert: 64 (over z, core).
Axes of the slice: x: 2, y: 2, z: 32, core: 2. Of those that a mesh axis runs over, the one named last changes fastest.
The devices are a block of a 4x8x32 slice.
Arguments:
- tokens: bfloat16 [2, 16384, 2048], P(None, ('groups', 'expert')), parts along dimension 1, may hold values from -6 to 6
- route_ids: int32 [2, 16384, 2], P(None, ('groups', 'expert')), parts along dimension 1, may hold values from 0 to 63, as said below
- route_slots: int32 [2, 16384, 2], P(None, ('groups', 'expert')), parts along dimension 1, may hold values from 0 to 3, as said below
- mod_shift: float32 [8, 2048], P('groups'), parts along dimension 0, may hold values from -4 to 4
- mod_scale: float32 [8, 2048], P('groups'), parts along dimension 0, may hold values from -4 to 4
- mod_gate: float32 [8, 2048], P('groups'), parts along dimension 0, may hold values from 0.1 to 1.9
- guidance: float32 [4], P('groups'), parts along dimension 0, may hold values from 2 to 6
- router_weight: bfloat16 [2048, 64], replicated, may hold values from -0.125 to 0.125
- expert_gate: bfloat16 [64, 2048, 768], P('expert'), may hold values from -0.125 to 0.125
- expert_up: bfloat16 [64, 2048, 768], P('expert'), may hold values from -0.125 to 0.125
- expert_down: bfloat16 [64, 768, 2048], P('expert'), may hold values from -0.21875 to 0.21875
- shared_gate: bfloat16 [2048, 1408], P('expert'), may hold values from -0.125 to 0.125
- shared_up: bfloat16 [2048, 1408], P('expert'), may hold values from -0.125 to 0.125
- shared_down: bfloat16 [1408, 2048], P(None, 'expert'), may hold values from -0.15625 to 0.15625
- head_weight: bfloat16 [2048, 128], replicated, may hold values from -0.125 to 0.125
Outputs:
- hidden_out: bfloat16 [2, 16384, 2048], P(None, ('groups', 'expert')), parts along dimension 1
- guided: float32 [16384, 128], P(('groups', 'expert')), parts along dimension 0
There are 4 independent parts, one for each index of `groups`. A program takes and returns all parts, laid end to end along the dimension named above; an argument that names none is the same for every part. Nothing has to cross between parts.
Inputs may be any that keep to these rules, and one draw needn't show every extreme that they name: `route_ids`: for each half, the 64 tokens of one device name each expert at most 4 times in all; this is met by some expert on every device, and one expert is named 4 times by every device's tokens of both halves. A token's 2 experts differ. `route_slots`: within one half and one device, the choices that name one expert hold the distinct rows 0 to their number minus 1, in the same place as the expert in route_ids.
All inputs are finite; a program needn't handle non-finite values.
Results may differ from a plain program's by a relative error of at most 0.0067.
Values may be sent and summed in bfloat16 or wider, within the bound.
No kernel may reach another device: no remote copies, remote signals or barrier semaphores. Data moves between devices by JAX's collectives and lax.ppermute only.
A program may use at most 128 MiB of HBM per device.

v0:
```python
import math

import jax
import jax.numpy as jnp
from jax import lax
from jax.sharding import PartitionSpec as P

epsilon = 1e-06


def gather_turned(arrays, axis, dims):
    turned = [jnp.moveaxis(a, dim, 0) for a, dim in zip(arrays, dims)]
    both = jnp.concatenate([t.reshape(len(t), -1) for t in turned], axis=1)
    result, at, gathered = (lax.all_gather(both, axis, axis=0, tiled=True), 0, [])
    for t, dim in zip(turned, dims):
        section = result[:, at : at + t[0].size].reshape(-1, *t.shape[1:])
        gathered.append(jnp.moveaxis(section, 0, dim))
        at += t[0].size
    return tuple(gathered)


def layer_norm(values):
    center = values - jnp.mean(values, axis=-1, keepdims=True)
    spread = jnp.mean(center * center, axis=-1, keepdims=True)
    return center * lax.rsqrt(spread + epsilon)


def expert_block(received, w_gate, w_up, w_down):
    array_shape = received.shape
    local_count = w_gate.shape[0]
    middle = math.prod(array_shape[1:-1])
    row_block = received.reshape(
        array_shape[0] // local_count, local_count, middle, array_shape[-1]
    )
    gate_part = jnp.einsum("semd,edf->semf", row_block, w_gate, preferred_element_type=jnp.float32)
    up_part = jnp.einsum("semd,edf->semf", row_block, w_up, preferred_element_type=jnp.float32)
    hidden = (jax.nn.silu(gate_part) * up_part).astype(jnp.bfloat16)
    result = jnp.einsum("semf,efd->semd", hidden, w_down, preferred_element_type=jnp.float32)
    return result.astype(jnp.bfloat16).reshape(array_shape)


def dispatch_matrix(slot_place, slot_total):
    slot_index = jnp.arange(slot_total, dtype=jnp.int32)
    matches = slot_index[:, None, None] == slot_place[None, :, :]
    return jnp.sum(matches.astype(jnp.int32), axis=2).astype(jnp.bfloat16)


def local(
    tokens,
    route_ids,
    route_slots,
    mod_shift,
    mod_scale,
    mod_gate,
    guidance,
    router_weight,
    expert_gate,
    expert_up,
    expert_down,
    shared_gate,
    shared_up,
    shared_down,
    head_weight,
):
    model_width = tokens.shape[-1]
    per_half = tokens.shape[1]
    choices_each = route_ids.shape[2]
    experts = router_weight.shape[1]
    capacity = 2 * choices_each * per_half // experts
    inputs = tokens.astype(jnp.float32)
    modulated = (layer_norm(inputs) * (1.0 + mod_scale[:, None, :]) + mod_shift[:, None, :]).astype(
        jnp.bfloat16
    )
    flat_rows = modulated.reshape(2 * per_half, model_width)
    logits = jnp.dot(flat_rows, router_weight, preferred_element_type=jnp.float32).reshape(
        2, per_half, experts
    )
    picked = jnp.take_along_axis(logits, route_ids, axis=2)
    affinity = jax.nn.sigmoid(picked)
    weights = affinity / jnp.sum(affinity, axis=2, keepdims=True)
    full_gate, full_up, full_down = gather_turned(
        (shared_gate, shared_up, shared_down), "expert", (0, 0, 1)
    )
    gate_sum = jnp.dot(flat_rows, full_gate, preferred_element_type=jnp.float32)
    up_sum = jnp.dot(flat_rows, full_up, preferred_element_type=jnp.float32)
    shared_hidden = (jax.nn.silu(gate_sum) * up_sum).astype(jnp.bfloat16)
    shared = jnp.dot(shared_hidden, full_down, preferred_element_type=jnp.float32)
    shared = shared.reshape(2, per_half, model_width)
    half_index = jnp.arange(2, dtype=jnp.int32)
    slot_place = (route_ids * 2 + half_index[:, None, None]) * capacity + route_slots
    matrix = dispatch_matrix(slot_place.reshape(2 * per_half, choices_each), 2 * experts * capacity)
    outgoing = jnp.dot(matrix, flat_rows, preferred_element_type=jnp.float32).astype(jnp.bfloat16)
    outgoing = outgoing.reshape(experts, 2, capacity, model_width)
    answered = expert_block(
        lax.all_to_all(outgoing, "expert", split_axis=0, concat_axis=0, tiled=True),
        expert_gate,
        expert_up,
        expert_down,
    )
    returned = lax.all_to_all(answered, "expert", split_axis=0, concat_axis=0, tiled=True)
    chosen = jnp.take(returned.reshape(-1, model_width), slot_place.reshape(-1), axis=0)
    chosen = chosen.reshape(2, per_half, choices_each, model_width)
    routed = jnp.sum(weights[..., None] * chosen.astype(jnp.float32), axis=2)
    hidden_out = (inputs + mod_gate[:, None, :] * (routed + shared)).astype(jnp.bfloat16)
    final_norm = layer_norm(hidden_out.astype(jnp.float32)).astype(jnp.bfloat16)
    predicted = jnp.dot(
        final_norm.reshape(2 * per_half, model_width),
        head_weight,
        preferred_element_type=jnp.float32,
    )
    predicted = predicted.reshape(2, per_half, head_weight.shape[1])
    guided = predicted[1] + guidance[0] * (predicted[0] - predicted[1])
    return (hidden_out, guided)


def solution(mesh):
    in_specs = (
        P(None, ("groups", "expert"), None),
        P(None, ("groups", "expert"), None),
        P(None, ("groups", "expert"), None),
        P("groups", None),
        P("groups", None),
        P("groups", None),
        P("groups"),
        P(),
        P("expert", None, None),
        P("expert", None, None),
        P("expert", None, None),
        P("expert", None),
        P("expert", None),
        P(None, "expert"),
        P(),
    )
    out_specs = (P(None, ("groups", "expert"), None), P(("groups", "expert"), None))
    return jax.shard_map(local, mesh=mesh, in_specs=in_specs, out_specs=out_specs, check_vma=False)
```

profile of v0, /device:TPU:38, one launch (start us, length us, event | category | flops | bytes accessed | tf_op | source)
XLA Modules:
  0.0 566.0 jit_solution(10287903076177642769)
XLA Ops:
  7.2 1.3 convert_reduce_fusion
  8.5 1.3 fusion.39
  9.9 0.7 compare_and_fusion
  10.7 0.7 broadcast_add_fusion
  11.5 1.4 fusion.42
  12.9 0.8 copy-done.1
  13.7 2.0 convolution_convert_fusion
  15.8 4.1 reshape.145
  19.9 34.4 %all-to-all-start = ((bf16[64,2,4,2048]{3,2,1,0:T(4,128)(2,1)}), bf16[64,2,4,2048]{3,2,1,0:T(4,128)(2,1)}, u32[]{:S(2)}, u32[]{:S(2)}) async-start(bf16[64,2,4,2048]{3,2,1,0:T(4,128)(2,1)} %reshape.145), calls=%async_computation | async-start | bytes 4194304 | tf_op jit(solution)/shard_map/all_to_all | solution.py:95
  54.4 0.7 pad_maximum_fusion
  55.2 217.1 %all-to-all-done = bf16[64,2,4,2048]{3,2,1,0:T(4,128)(2,1)} async-done(((bf16[64,2,4,2048]{3,2,1,0:T(4,128)(2,1)}), bf16[64,2,4,2048]{3,2,1,0:T(4,128)(2,1)}, u32[]{:S(2)}, u32[]{:S(2)}) %all-to-all-start) | async-done | bytes 2097184 | tf_op jit(solution)/shard_map/all_to_all | solution.py:95
  272.3 4.0 reshape.146
  276.3 5.6 fusion.10
  281.9 8.3 %fusion.15 = bf16[64,1,8,2048]{3,2,0,1:T(8,128)(2,1)} fusion(bf16[1,768,2048]{2,1,0:T(8,128)(2,1)S(1)} %copy-done, bf16[64,8,2048]{2,1,0:T(8,128)(2,1)} %reshape.146, bf16[1,2048,768]{2,1,0:T(8,128)(2,1)} %param.24, f32[64,8,768]{2,1,0:T(8,128)} %fusion.10), kind=kOutput, calls=%fused_computation.16 | convolution fusion | flops 3224633344 | bytes 12058624 | tf_op jit(solution)/shard_map/semf,efd->semd/dot_general | solution.py:38
  290.2 4.1 reshape.151
  294.4 7.5 %all-to-all-start.1 = ((bf16[64,2,4,2048]{3,2,1,0:T(4,128)(2,1)}), bf16[64,2,4,2048]{3,2,1,0:T(4,128)(2,1)}, u32[]{:S(2)}, u32[]{:S(2)}) async-start(bf16[64,2,4,2048]{3,2,1,0:T(4,128)(2,1)} %reshape.151), calls=%async_computation.1 | async-start | bytes 4194304 | tf_op jit(solution)/shard_map/all_to_all | solution.py:100
  302.8 0.1 reshape.153
  303.0 0.1 reshape.164
  303.2 1.3 fusion.54
  304.6 2.4 gather_fusion.1
  307.4 215.9 %all-to-all-done.1 = bf16[64,2,4,2048]{3,2,1,0:T(4,128)(2,1)} async-done(((bf16[64,2,4,2048]{3,2,1,0:T(4,128)(2,1)}), bf16[64,2,4,2048]{3,2,1,0:T(4,128)(2,1)}, u32[]{:S(2)}, u32[]{:S(2)}) %all-to-all-start.1) | async-done | bytes 2097184 | tf_op jit(solution)/shard_map/all_to_all | solution.py:100
  523.3 4.0 reshape.152
  527.3 5.2 gather_fusion
  532.5 2.5 gather.12
  535.0 7.2 %multiply_reduce_fusion = f32[2,64,2048]{2,1,0:T(8,128)} fusion(bf16[2,64,2,2048]{3,2,1,0:T(2,128)(2,1)} %gather.12, pred[2,64,2]{2,1,0:T(8,128)(4,1)S(1)} %copy.43, f32[2,64,2]{2,1,0:T(8,128)S(1)} %copy.42), kind=kLoop, calls=%fused_computation.19 | loop fusion | flops 1835008 | bytes 2098432 | tf_op jit(solution)/shard_map/reduce_sum | solution.py:103
  542.3 4.7 fusion.4
  547.0 8.6 %fusion = f32[128,2048]{1,0:T(8,128)} fusion(bf16[2048,4224]{1,0:T(8,128)(2,1)} %all-gather.2.cloned.1.call-done, bf16[128,2048]{1,0:T(8,128)(2,1)} %bitcast.97, f32[128,1408]{1,0:T(8,128)} %fusion.4), kind=kOutput, calls=%fused_computation.2 | convolution fusion | flops 1477476352 | bytes 13828096 | tf_op jit(solution)/shard_map/dot_general | solution.py:87
  555.5 2.0 convert_reduce_fusion.1
  557.5 0.3 fusion.43
  557.8 0.3 fusion.44
  558.2 0.3 fusion.63
  558.5 0.6 fusion.58
  (40 shorter events, 1.0 us)
Async XLA Ops:
  7.2 274.7 %copy-start = (bf16[1,768,2048]{2,1,0:T(8,128)(2,1)S(1)}, bf16[1,768,2048]{2,1,0:T(8,128)(2,1)}, u32[]{:S(2)}) copy-start(bf16[1,768,2048]{2,1,0:T(8,128)(2,1)} %param.25) | copy-start | bytes 9437188
  12.9 0.8 copy-start.1
  19.9 34.5 %copy-start.5 = (bf16[1408,32]{0,1:T(8,128)(2,1)S(1)}, bf16[1408,32]{0,1:T(8,128)(2,1)}, u32[]{:S(2)}) copy-start(bf16[1408,32]{0,1:T(8,128)(2,1)} %param.28) | copy-start | bytes 270340
  19.9 34.5 %copy-start.6 = (bf16[32,1408]{1,0:T(8,128)(2,1)S(1)}, bf16[32,1408]{1,0:T(8,128)(2,1)}, u32[]{:S(2)}) copy-start(bf16[32,1408]{1,0:T(8,128)(2,1)} %param.27) | copy-start | bytes 270340
  19.9 34.5 %copy-start.7 = (bf16[32,1408]{1,0:T(8,128)(2,1)S(1)}, bf16[32,1408]{1,0:T(8,128)(2,1)}, u32[]{:S(2)}) copy-start(bf16[32,1408]{1,0:T(8,128)(2,1)} %param.26) | copy-start | bytes 270340
  19.9 252.4 %all-to-all-start = ((bf16[64,2,4,2048]{3,2,1,0:T(4,128)(2,1)}), bf16[64,2,4,2048]{3,2,1,0:T(4,128)(2,1)}, u32[]{:S(2)}, u32[]{:S(2)}) async-start(bf16[64,2,4,2048]{3,2,1,0:T(4,128)(2,1)} %reshape.145), calls=%async_computation | async-start | bytes 4194304 | tf_op jit(solution)/shard_map/all_to_all | solution.py:95
  54.3 488.0 %all-gather.2.cloned.1.call-start = ((), (), s32[]{:S(2)}) async-start(), calls=%async_computation.2 | async-start | bytes 17571840 | tf_op jit(solution)/shard_map/all_gather | solution.py:14
  294.4 8.6 %copy-start.8 = (s32[2,64,2]{1,2,0:T(2,128)S(1)}, s32[2,64,2]{1,2,0:T(2,128)}, u32[]{:S(2)}) copy-start(s32[2,64,2]{1,2,0:T(2,128)} %param.16) | copy-start | bytes 3076
  294.4 8.8 %copy-start.4 = (bf16[2048,64]{0,1:T(8,128)(2,1)S(1)}, bf16[2048,64]{0,1:T(8,128)(2,1)}, u32[]{:S(2)}) copy-start(bf16[2048,64]{0,1:T(8,128)(2,1)} %param.22) | copy-start | bytes 786436
  294.4 229.0 %all-to-all-start.1 = ((bf16[64,2,4,2048]{3,2,1,0:T(4,128)(2,1)}), bf16[64,2,4,2048]{3,2,1,0:T(4,128)(2,1)}, u32[]{:S(2)}, u32[]{:S(2)}) async-start(bf16[64,2,4,2048]{3,2,1,0:T(4,128)(2,1)} %reshape.151), calls=%async_computation.1 | async-start | bytes 4194304 | tf_op jit(solution)/shard_map/all_to_all | solution.py:100
  547.0 8.6 %copy-start.9 = (f32[2,2048]{1,0:T(2,128)S(1)}, f32[2,2048]{1,0:T(2,128)}, u32[]{:S(2)}) copy-start(f32[2,2048]{1,0:T(2,128)} %param.20) | copy-start | bytes 49156
  555.5 2.6 copy-start.3
  557.5 1.6 copy-start.2
Sparse Core Ops, SparseCore 0:
  57.0 467.0 all-gather.1
where the time goes:
time: 567 us; the launch traced here: 566 us
  waiting for transfers between devices  433 us (76%)
  starting transfers between devices  42 us (7%)
  matrix products  30.9 us (5%)
  local copies, waits for them, and re-layouts  28.2 us (5%)
  other arithmetic  16.9 us (3%)
  between operations  14.9 us (3%)
    all_to_all x1, waiting for transfers between devices, local(): lax.all_to_all(outgoing, 'expert', split_axis=0, concat_axis=0, tiled=True)  217 us
    all_to_all x1, waiting for transfers between devices, local(): lax.all_to_all(answered, 'expert', split_axis=0, concat_axis=0, tiled=True)  216 us
    all_to_all x1, starting transfers between devices, local(): lax.all_to_all(outgoing, 'expert', split_axis=0, concat_axis=0, tiled=True)  34.4 us
  transfers between devices with their start and end apart: 3, of which 2 were waited for; matrix products, arithmetic and copies ran while one was open for 8% of the time, Pallas kernels for 0%

commit v1 on v0

v1 whole, which is shorter than its diff:
```python
import jax
import jax.numpy as jnp
from jax import lax
from jax.sharding import PartitionSpec as P

epsilon = 1e-06
lanes = 2


def gather_turned(arrays, axis, dims):
    turned = [jnp.moveaxis(a, dim, 0) for a, dim in zip(arrays, dims)]
    both = jnp.concatenate([t.reshape(len(t), -1) for t in turned], axis=1)
    result, at, gathered = (lax.all_gather(both, axis, axis=0, tiled=True), 0, [])
    for t, dim in zip(turned, dims):
        section = result[:, at : at + t[0].size].reshape(-1, *t.shape[1:])
        gathered.append(jnp.moveaxis(section, 0, dim))
        at += t[0].size
    return tuple(gathered)


def layer_norm(values):
    center = values - jnp.mean(values, axis=-1, keepdims=True)
    spread = jnp.mean(center * center, axis=-1, keepdims=True)
    return center * lax.rsqrt(spread + epsilon)


def mm(a, b):
    return jnp.dot(a, b, preferred_element_type=jnp.float32)


def mm_turned(a, b):
    return lax.dot_general(a, b, (((0,), (0,)), ((), ())), preferred_element_type=jnp.float32)


def descending_rank(extent):
    index = jnp.arange(extent.shape[0], dtype=jnp.int32)
    ahead = (extent[None, :] > extent[:, None]) | (
        (extent[None, :] == extent[:, None]) & (index[None, :] < index[:, None])
    )
    return jnp.sum(ahead.astype(jnp.int32), axis=1)


def build(devices):
    ring = devices // lanes
    reach = ring // 2

    def local(
        tokens,
        route_ids,
        route_slots,
        mod_shift,
        mod_scale,
        mod_gate,
        guidance,
        router_weight,
        expert_gate,
        expert_up,
        expert_down,
        shared_gate,
        shared_up,
        shared_down,
        head_weight,
    ):
        width = tokens.shape[-1]
        per_half = tokens.shape[1]
        rows = 2 * per_half
        choices = route_ids.shape[2]
        experts = router_weight.shape[1]
        capacity = 2 * choices * per_half // experts
        slots = 2 * capacity
        assert experts == devices and expert_gate.shape[0] == 1
        limits = [min(rows, slots * (lanes * (reach - hop) + 1)) for hop in range(reach + 1)]
        column = width // 2
        columns = [slice(0, column), slice(column, width)]

        def shift(values, step):
            pairs = [
                (lanes * z + c, lanes * ((z + step) % ring) + c)
                for z in range(ring)
                for c in range(lanes)
            ]
            return lax.ppermute(values, "expert", pairs)

        def swap(values):
            return lax.ppermute(values, "expert", [(i, i ^ 1) for i in range(devices)])

        full_gate, full_up, full_down = gather_turned(
            (shared_gate, shared_up, shared_down), "expert", (0, 0, 1)
        )

        inputs = tokens.astype(jnp.float32)
        modulated = (
            layer_norm(inputs) * (1.0 + mod_scale[:, None, :]) + mod_shift[:, None, :]
        ).astype(jnp.bfloat16)
        flat = modulated.reshape(rows, width)

        me = lax.axis_index("expert")
        chip, core = me // lanes, me % lanes
        ids = route_ids.reshape(rows, choices)
        half = jnp.arange(rows, dtype=jnp.int32)[:, None] // per_half
        place = (ids * 2 + half) * capacity + route_slots.reshape(rows, choices)
        ahead = (ids // lanes - chip) % ring
        upward = ((ahead >= 1) & (ahead < reach)) | ((ahead == reach) & (ids % lanes == 0))
        downward = (ahead > reach) | ((ahead == reach) & (ids % lanes != 0))
        up_rank = descending_rank(jnp.max(jnp.where(upward, ahead, 0), axis=1))
        down_rank = descending_rank(jnp.max(jnp.where(downward, ring - ahead, 0), axis=1))
        order = jnp.arange(rows, dtype=jnp.int32)
        up_matrix = (order[:, None] == up_rank[None, :]).astype(jnp.bfloat16)
        down_matrix = (order[:, None] == down_rank[None, :]).astype(jnp.bfloat16)
        at = jnp.where(
            upward, up_rank[:, None], jnp.where(downward, down_rank[:, None], order[:, None])
        )

        up_rows = mm(up_matrix, flat).astype(jnp.bfloat16)
        down_rows = mm(down_matrix, flat).astype(jnp.bfloat16)

        logits = mm(flat, router_weight)
        expert_index = jnp.arange(experts, dtype=jnp.int32)
        picked = jnp.sum(
            jnp.where(expert_index == ids[:, :, None], logits[:, None, :], 0.0), axis=2
        )
        affinity = jax.nn.sigmoid(picked)
        weights = affinity / jnp.sum(affinity, axis=1, keepdims=True)

        slot_index = jnp.arange(experts * slots, dtype=jnp.int32)
        matches = slot_index[:, None] == place.reshape(1, rows * choices)
        slot_at = jnp.sum(
            jnp.where(matches, (at + 1).astype(jnp.float32).reshape(1, -1), 0.0), axis=1
        )
        slot_weight = jnp.sum(jnp.where(matches, weights.reshape(1, -1), 0.0), axis=1)
        per_chip = lanes * slots
        line = jnp.concatenate(
            [slot_at.reshape(ring, per_chip) - 1.0, slot_weight.reshape(ring, per_chip)], axis=1
        )
        line = jnp.pad(line, ((0, 0), (0, 128 - 2 * per_chip)))
        line = jnp.broadcast_to(line[:, None, :], (ring, lanes, 128)).reshape(devices, 128)
        table = lax.all_to_all(line, "expert", split_axis=0, concat_axis=0, tiled=True)

        back = jnp.arange(ring, dtype=jnp.int32)
        source = lanes * ((chip - back) % ring)
        table = jnp.take(table, jnp.concatenate([source + core, source + 1 - core]), axis=0)
        mine = table[:ring]

        def own_first(values):
            values = values.reshape(ring, lanes, slots)
            return jnp.where(core == 0, values, values[:, ::-1])

        wanted = own_first(mine[:, :per_chip]).reshape(ring, per_chip)
        pick = (wanted[:, :, None] == order.astype(jnp.float32)).astype(jnp.bfloat16)
        core_of = jnp.where(jnp.arange(per_chip, dtype=jnp.int32) < slots, core, 1 - core)
        own_weight = own_first(mine[:, per_chip : 2 * per_chip])[:, 0]
        other_weight = table[ring:, per_chip : 2 * per_chip].reshape(ring, lanes, slots)
        other_weight = jnp.where(core == 0, other_weight[:, 0], other_weight[:, 1])

        far_up = jnp.where(core_of[:, None] == 0, pick[reach], 0)
        far_down = jnp.where(core_of[:, None] != 0, pick[reach], 0)

        def up_pick(hop):
            return (far_up if hop == reach else pick[hop])[:, : limits[hop]]

        def down_pick(hop):
            return (far_down if hop == reach else pick[ring - hop])[:, : limits[hop]]

        taken = {0: mm(pick[0], flat).astype(jnp.bfloat16)}
        ups = [up_rows[:, c] for c in columns]
        downs = [down_rows[:, c] for c in columns]
        for hop in range(1, reach + 1):
            for i in range(len(columns)):
                ups[i] = shift(ups[i][: limits[hop]], 1)
                downs[i] = shift(downs[i][: limits[hop]], -1)
            up_part = [mm(up_pick(hop), v) for v in ups]
            down_part = [mm(down_pick(hop), v) for v in downs]
            if hop < reach:
                taken[hop] = jnp.concatenate(up_part, axis=1).astype(jnp.bfloat16)
                taken[ring - hop] = jnp.concatenate(down_part, axis=1).astype(jnp.bfloat16)
            else:
                both = [u + d for u, d in zip(up_part, down_part)]
                taken[hop] = jnp.concatenate(both, axis=1).astype(jnp.bfloat16)

        near = [o for o in range(ring) if min(o, ring - o) <= reach // 2]
        far = [o for o in range(ring) if min(o, ring - o) > reach // 2]
        answer = {}
        for batch in (near, far):
            stacked = jnp.stack([taken[o] for o in batch])
            own, other = stacked[:, :slots], swap(stacked[:, slots:])
            block = jnp.concatenate([own, other]).reshape(-1, width)
            gate_part = mm(block, expert_gate[0])
            up_part = mm(block, expert_up[0])
            hidden = (jax.nn.silu(gate_part) * up_part).astype(jnp.bfloat16)
            result = mm(hidden, expert_down[0])
            scale = jnp.concatenate(
                [
                    jnp.stack([own_weight[o] for o in batch]),
                    jnp.stack([other_weight[o] for o in batch]),
                ]
            )
            result = (result.reshape(-1, slots, width) * scale[:, :, None]).astype(jnp.bfloat16)
            own, other = result[: len(batch)], swap(result[len(batch) :])
            both = jnp.concatenate([own, other], axis=1)
            for i, o in enumerate(batch):
                answer[o] = both[i]

        up_sum, down_sum = [None, None], [None, None]
        for hop in range(reach, 0, -1):
            for sums, chosen, o, step in (
                (up_sum, up_pick(hop), hop, -1),
                (down_sum, down_pick(hop), ring - hop, 1),
            ):
                for i, c in enumerate(columns):
                    total = mm_turned(chosen, answer[o][:, c])
                    if sums[i] is not None:
                        short = limits[hop] - sums[i].shape[0]
                        total = total + jnp.pad(sums[i], ((0, short), (0, 0))).astype(jnp.float32)
                    sums[i] = shift(total.astype(jnp.bfloat16), step)
        routed = (
            mm_turned(pick[0], answer[0])
            + jnp.concatenate([mm_turned(up_matrix[: limits[1]], v) for v in up_sum], axis=1)
            + jnp.concatenate([mm_turned(down_matrix[: limits[1]], v) for v in down_sum], axis=1)
        ).reshape(2, per_half, width)

        gate_sum = mm(flat, full_gate)
        up_sum = mm(flat, full_up)
        shared_hidden = (jax.nn.silu(gate_sum) * up_sum).astype(jnp.bfloat16)
        shared = mm(shared_hidden, full_down).reshape(2, per_half, width)

        hidden_out = (inputs + mod_gate[:, None, :] * (routed + shared)).astype(jnp.bfloat16)
        final_norm = layer_norm(hidden_out.astype(jnp.float32)).astype(jnp.bfloat16)
        predicted = mm(final_norm.reshape(rows, width), head_weight)
        predicted = predicted.reshape(2, per_half, head_weight.shape[1])
        guided = predicted[1] + guidance[0] * (predicted[0] - predicted[1])
        return (hidden_out, guided)

    return local


def solution(mesh):
    in_specs = (
        P(None, ("groups", "expert"), None),
        P(None, ("groups", "expert"), None),
        P(None, ("groups", "expert"), None),
        P("groups", None),
        P("groups", None),
        P("groups", None),
        P("groups"),
        P(),
        P("expert", None, None),
        P("expert", None, None),
        P("expert", None, None),
        P("expert", None),
        P("expert", None),
        P(None, "expert"),
        P(),
    )
    out_specs = (P(None, ("groups", "expert"), None), P(("groups", "expert"), None))
    local = build(mesh.shape["expert"])
    return jax.shard_map(local, mesh=mesh, in_specs=in_specs, out_specs=out_specs, check_vma=False)
```

time: 567 us -> 523 us (0.922); the launches traced: 566 us -> 514 us
  waiting for transfers between devices: 433 us -> 153 us
  starting transfers between devices: 42 us -> 239 us
  matrix products: 30.9 us -> 66.9 us
    all_to_all x2 -> x1, waiting for transfers between devices: 433 us -> 11.8 us  [local(): lax.all_to_all(line, 'expert', split_axis=0, concat_axis=0, tiled=True)]
    ppermute x0 -> x132, starting transfers between devices: none -> 204 us  [the longest x128 203 us: shift(): return lax.ppermute(values, 'expert', pairs)]
    ppermute x0 -> x132, waiting for transfers between devices: none -> 141 us  [the longest x128 141 us: shift(): return lax.ppermute(values, 'expert', pairs)]
    dot_general x7 -> x144, matrix products: 30.9 us -> 66.9 us  [the longest x75 45.3 us: mm(): return jnp.dot(a, b, preferred_element_type=jnp.float32)]
    reshape x4 -> x3, local copies, waits for them, and re-layouts: 12.4 us -> 0.88 us  [the longest x1 0.67 us: local(): place = (ids * 2 + half) * capacity + route_slots.reshape(rows, choices)]
    gather x7 -> x1, local copies, waits for them, and re-layouts: 10.6 us -> 0.6 us  [local(): jnp.take(table, jnp.concatenate([source + core, source + 1 - core]), axis=0)]
    slice x0 -> x47, local copies, waits for them, and re-layouts: none -> 9.89 us  [the longest x2 3.77 us: local(): own, other = (result[:len(batch)], swap(result[len(batch):]))]
    all_to_all x2 -> x1, starting transfers between devices: 41.9 us -> 34.2 us  [local(): lax.all_to_all(line, 'expert', split_axis=0, concat_axis=0, tiled=True)]
  transfers between devices with their start and end apart: 3 -> 134, of which waited for: 2 -> 44; matrix products, arithmetic and copies ran while one was open for 8% -> 17% of each run, Pallas kernels for 0% -> 0%
where the time goes in v1:
time: 523 us; the launch traced here: 514 us
  starting transfers between devices  239 us (46%)
  waiting for transfers between devices  153 us (29%)
  matrix products  66.9 us (13%)
  local copies, waits for them, and re-layouts  22.8 us (4%)
  between operations  16.8 us (3%)
  other arithmetic  16.2 us (3%)
    ppermute x128, starting transfers between devices, shift(): return lax.ppermute(values, 'expert', pairs)  203 us
    ppermute x128, waiting for transfers between devices, shift(): return lax.ppermute(values, 'expert', pairs)  141 us
    dot_general x75, matrix products, mm(): return jnp.dot(a, b, preferred_element_type=jnp.float32)  45.3 us
    all_to_all x1, starting transfers between devices, local(): lax.all_to_all(line, 'expert', split_axis=0, concat_axis=0, tiled=True)  34.2 us
    dot_general x69, matrix products, mm_turned(): lax.dot_general(a, b, (((0,), (0,)), ((), ())), preferred_element_type=jn...  21.5 us
    all_to_all x1, waiting for transfers between devices, local(): lax.all_to_all(line, 'expert', split_axis=0, concat_axis=0, tiled=True)  11.8 us
  transfers between devices with their start and end apart: 134, of which 44 were waited for; matrix products, arithmetic and copies ran while one was open for 17% of the time, Pallas kernels for 0%

profile of v1, /device:TPU:38, one launch (start us, length us, event | category | flops | bytes accessed | tf_op | source)
XLA Modules:
  0.0 514.2 jit_solution(16707751281748719403)
XLA Ops:
  25.5 34.2 %all-to-all-start = ((f32[64,1,128]{2,1,0:T(1,128)}), f32[64,1,128]{2,1,0:T(1,128)S(1)}, u32[]{:S(2)}, u32[]{:S(2)}) async-start(f32[64,1,128]{2,1,0:T(1,128)} %bitcast.1), calls=%async_computation | async-start | bytes 65536 | tf_op jit(solution)/shard_map/all_to_all | solution.py:137
  70.2 11.8 %all-to-all-done = f32[64,1,128]{2,1,0:T(1,128)S(1)} async-done(((f32[64,1,128]{2,1,0:T(1,128)}), f32[64,1,128]{2,1,0:T(1,128)S(1)}, u32[]{:S(2)}, u32[]{:S(2)}) %all-to-all-start) | async-done | bytes 32800 | tf_op jit(solution)/shard_map/all_to_all | solution.py:137
  100.8 6.4 %collective-permute-done.3 = bf16[128,1024]{1,0:T(8,128)(2,1)S(1)} collective-permute-done((bf16[128,1024]{1,0:T(8,128)(2,1)}, bf16[128,1024]{1,0:T(8,128)(2,1)S(1)}, u32[]{:S(2)}, u32[]{:S(2)}) %collective-permute-start.3) | collective-permute-done | bytes 262176 | tf_op jit(solution)/shard_map/ppermute | solution.py:82
  107.4 11.1 %collective-permute-done.2 = bf16[128,1024]{1,0:T(8,128)(2,1)S(1)} collective-permute-done((bf16[128,1024]{1,0:T(8,128)(2,1)}, bf16[128,1024]{1,0:T(8,128)(2,1)S(1)}, u32[]{:S(2)}, u32[]{:S(2)}) %collective-permute-start.2) | collective-permute-done | bytes 262176 | tf_op jit(solution)/shard_map/ppermute | solution.py:82
  123.5 6.2 %collective-permute-done.5 = bf16[128,1024]{1,0:T(8,128)(2,1)S(1)} collective-permute-done((bf16[128,1024]{1,0:T(8,128)(2,1)S(1)}, bf16[128,1024]{1,0:T(8,128)(2,1)S(1)}, u32[]{:S(2)}, u32[]{:S(2)}) %collective-permute-start.5) | collective-permute-done | bytes 262176 | tf_op jit(solution)/shard_map/ppermute | solution.py:82
  129.8 11.1 %collective-permute-done.4 = bf16[128,1024]{1,0:T(8,128)(2,1)S(1)} collective-permute-done((bf16[128,1024]{1,0:T(8,128)(2,1)S(1)}, bf16[128,1024]{1,0:T(8,128)(2,1)S(1)}, u32[]{:S(2)}, u32[]{:S(2)}) %collective-permute-start.4) | collective-permute-done | bytes 262176 | tf_op jit(solution)/shard_map/ppermute | solution.py:82
  146.5 5.6 %collective-permute-done.7 = bf16[128,1024]{1,0:T(8,128)(2,1)S(1)} collective-permute-done((bf16[128,1024]{1,0:T(8,128)(2,1)S(1)}, bf16[128,1024]{1,0:T(8,128)(2,1)S(1)}, u32[]{:S(2)}, u32[]{:S(2)}) %collective-permute-start.7) | collective-permute-done | bytes 262176 | tf_op jit(solution)/shard_map/ppermute | solution.py:82
  152.2 11.2 %collective-permute-done.6 = bf16[128,1024]{1,0:T(8,128)(2,1)S(1)} collective-permute-done((bf16[128,1024]{1,0:T(8,128)(2,1)S(1)}, bf16[128,1024]{1,0:T(8,128)(2,1)S(1)}, u32[]{:S(2)}, u32[]{:S(2)}) %collective-permute-start.6) | collective-permute-done | bytes 262176 | tf_op jit(solution)/shard_map/ppermute | solution.py:82
  169.2 5.5 %collective-permute-done.9 = bf16[128,1024]{1,0:T(8,128)(2,1)S(1)} collective-permute-done((bf16[128,1024]{1,0:T(8,128)(2,1)S(1)}, bf16[128,1024]{1,0:T(8,128)(2,1)S(1)}, u32[]{:S(2)}, u32[]{:S(2)}) %collective-permute-start.9) | collective-permute-done | bytes 262176 | tf_op jit(solution)/shard_map/ppermute | solution.py:82
  174.6 11.2 %collective-permute-done.8 = bf16[128,1024]{1,0:T(8,128)(2,1)S(1)} collective-permute-done((bf16[128,1024]{1,0:T(8,128)(2,1)S(1)}, bf16[128,1024]{1,0:T(8,128)(2,1)S(1)}, u32[]{:S(2)}, u32[]{:S(2)}) %collective-permute-start.8) | collective-permute-done | bytes 262176 | tf_op jit(solution)/shard_map/ppermute | solution.py:82
  185.9 11.9 %collective-permute-start.29 = (bf16[128,1024]{1,0:T(8,128)(2,1)S(1)}, bf16[128,1024]{1,0:T(8,128)(2,1)S(1)}, u32[]{:S(2)}, u32[]{:S(2)}) collective-permute-start(bf16[128,1024]{1,0:T(8,128)(2,1)S(1)} %collective-permute-done.28), channel_id=1, source_target_pairs={{0,62},{1,63},{2,0},{3,1},{4,2},{5,3},{6,4},{7,5},{8,6},{9,7},{10,... | collective-permute-start | bytes 786440 | tf_op jit(solution)/shard_map/ppermute | solution.py:82
  200.5 7.8 %collective-permute-done.10 = bf16[128,1024]{1,0:T(8,128)(2,1)S(1)} collective-permute-done((bf16[128,1024]{1,0:T(8,128)(2,1)S(1)}, bf16[128,1024]{1,0:T(8,128)(2,1)S(1)}, u32[]{:S(2)}, u32[]{:S(2)}) %collective-permute-start.10) | collective-permute-done | bytes 262176 | tf_op jit(solution)/shard_map/ppermute | solution.py:82
  209.9 3.7 collective-permute-start.30
  213.6 4.1 collective-permute-done.21
  217.6 3.7 collective-permute-start.22
  232.0 5.5 %collective-permute-done.14 = bf16[128,1024]{1,0:T(8,128)(2,1)S(1)} collective-permute-done((bf16[128,1024]{1,0:T(8,128)(2,1)S(1)}, bf16[128,1024]{1,0:T(8,128)(2,1)S(1)}, u32[]{:S(2)}, u32[]{:S(2)}) %collective-permute-start.14) | collective-permute-done | bytes 262176 | tf_op jit(solution)/shard_map/ppermute | solution.py:82
  254.4 4.4 collective-permute-done.36
  306.8 5.7 %fusion.24 = bf16[34,8,2048]{2,1,0:T(8,128)(2,1)} fusion(bf16[1,768,2048]{2,1,0:T(8,128)(2,1)S(1)} %copy-done, f32[34,8]{1,0:T(8,128)S(1)} %copy.218, bf16[1,2048,768]{2,1,0:T(8,128)(2,1)} %param.24, bf16[17,8,2048]{2,1,0:T(8,128)(2,1)} %copy-done.27, bf16[17,8,2048]{2,1,0:T(8,128)(2,1)} %copy-done.9, f32[272,768]{1,0:T(8,128)} %fusion.16), kind=kOutput, calls=%fused_computation.81 | convolution fusion | flops 1714200576 | bytes 9356352 | tf_op jit(solution)/shard_map/dot_general | solution.py:28
  315.4 3.9 fusion.14
  319.3 5.4 %fusion.27 = bf16[30,8,2048]{2,1,0:T(8,128)(2,1)} fusion(bf16[1,768,2048]{2,1,0:T(8,128)(2,1)S(1)} %copy-done, f32[30,8]{1,0:T(8,128)S(1)} %copy-done.14, bf16[1,2048,768]{2,1,0:T(8,128)(2,1)} %param.24, bf16[15,8,2048]{2,1,0:T(8,128)(2,1)} %collective-permute-done.66, bf16[15,8,2048]{2,1,0:T(8,128)(2,1)} %get-tuple-element.45, f32[240,768]{1,0:T(8,128)} %fusion.14), kind=kOutput, calls=%fused_computation.82 | convolution fusion | flops 1512529920 | bytes 8995776 | tf_op jit(solution)/shard_map/dot_general | solution.py:28
  360.6 3.5 collective-permute-start.89
  393.0 3.8 collective-permute-start.76
  405.3 3.8 collective-permute-start.77
  409.5 3.6 collective-permute-done.108
  420.7 4.7 collective-permute-done.109
  433.0 3.7 collective-permute-done.110
  441.2 3.7 collective-permute-start.80
  453.3 3.8 collective-permute-start.81
  464.8 3.8 collective-permute-start.82
  474.9 3.6 collective-permute-start.83
  490.6 3.6 fusion.4
  494.2 8.2 %fusion = f32[128,2048]{1,0:T(8,128)} fusion(bf16[2048,4224]{1,0:T(8,128)(2,1)} %all-gather.2.cloned.1.call-done, bf16[128,2048]{1,0:T(8,128)(2,1)S(1)} %bitcast.558, f32[128,1408]{1,0:T(8,128)S(1)} %fusion.4), kind=kOutput, calls=%fused_computation.1 | convolution fusion | flops 1477476352 | bytes 13828096 | tf_op jit(solution)/shard_map/dot_general | solution.py:28
  (584 shorter events, 277.2 us)
Async XLA Ops:
  7.2 483.4 %all-gather.2.cloned.1.call-start = ((), (), s32[]{:S(2)}) async-start(), calls=%async_computation.1 | async-start | bytes 17571840 | tf_op jit(solution)/shard_map/all_gather | solution.py:13
  25.5 56.5 %all-to-all-start = ((f32[64,1,128]{2,1,0:T(1,128)}), f32[64,1,128]{2,1,0:T(1,128)S(1)}, u32[]{:S(2)}, u32[]{:S(2)}) async-start(f32[64,1,128]{2,1,0:T(1,128)} %bitcast.1), calls=%async_computation | async-start | bytes 65536 | tf_op jit(solution)/shard_map/all_to_all | solution.py:137
  62.0 28.9 %collective-permute-start.1 = (bf16[128,1024]{1,0:T(8,128)(2,1)}, bf16[128,1024]{1,0:T(8,128)(2,1)}, u32[]{:S(2)}, u32[]{:S(2)}) collective-permute-start(bf16[128,1024]{1,0:T(8,128)(2,1)} %get-tuple-element.50), channel_id=1, source_target_pairs={{0,2},{1,3},{2,4},{3,5},{4,6},{5,7},{6,8},{7,9},{8,10},{9,11},{10,... | collective-permute-start | bytes 786440 | tf_op jit(solution)/shard_map/ppermute | solution.py:82
  62.7 30.1 %collective-permute-start = (bf16[128,1024]{1,0:T(8,128)(2,1)}, bf16[128,1024]{1,0:T(8,128)(2,1)}, u32[]{:S(2)}, u32[]{:S(2)}) collective-permute-start(bf16[128,1024]{1,0:T(8,128)(2,1)} %get-tuple-element.49), channel_id=1, source_target_pairs={{0,2},{1,3},{2,4},{3,5},{4,6},{5,7},{6,8},{7,9},{8,10},{9,11},{10,... | collective-permute-start | bytes 786440 | tf_op jit(solution)/shard_map/ppermute | solution.py:82
  65.3 29.3 %collective-permute-start.24 = (bf16[128,1024]{1,0:T(8,128)(2,1)}, bf16[128,1024]{1,0:T(8,128)(2,1)}, u32[]{:S(2)}, u32[]{:S(2)}) collective-permute-start(bf16[128,1024]{1,0:T(8,128)(2,1)} %get-tuple-element.48), channel_id=1, source_target_pairs={{0,62},{1,63},{2,0},{3,1},{4,2},{5,3},{6,4},{7,5},{8,6},{9,7},{10,... | collective-permute-start | bytes 786440 | tf_op jit(solution)/shard_map/ppermute | solution.py:82
  67.1 31.8 %collective-permute-start.16 = (bf16[128,1024]{1,0:T(8,128)(2,1)}, bf16[128,1024]{1,0:T(8,128)(2,1)S(1)}, u32[]{:S(2)}, u32[]{:S(2)}) collective-permute-start(bf16[128,1024]{1,0:T(8,128)(2,1)} %get-tuple-element.47), channel_id=1, source_target_pairs={{0,62},{1,63},{2,0},{3,1},{4,2},{5,3},{6,4},{7,5},{8,6},{9,7},{10,... | collective-permute-start | bytes 786440 | tf_op jit(solution)/shard_map/ppermute | solution.py:82
  90.9 16.3 %collective-permute-start.3 = (bf16[128,1024]{1,0:T(8,128)(2,1)}, bf16[128,1024]{1,0:T(8,128)(2,1)S(1)}, u32[]{:S(2)}, u32[]{:S(2)}) collective-permute-start(bf16[128,1024]{1,0:T(8,128)(2,1)} %collective-permute-done.1), channel_id=1, source_target_pairs={{0,2},{1,3},{2,4},{3,5},{4,6},{5,7},{6,8},{7,9},{8,10},{9,11},{10,... | collective-permute-start | bytes 786440 | tf_op jit(solution)/shard_map/ppermute | solution.py:82
  94.5 23.9 %collective-permute-start.2 = (bf16[128,1024]{1,0:T(8,128)(2,1)}, bf16[128,1024]{1,0:T(8,128)(2,1)S(1)}, u32[]{:S(2)}, u32[]{:S(2)}) collective-permute-start(bf16[128,1024]{1,0:T(8,128)(2,1)} %collective-permute-done), channel_id=1, source_target_pairs={{0,2},{1,3},{2,4},{3,5},{4,6},{5,7},{6,8},{7,9},{8,10},{9,11},{10,... | collective-permute-start | bytes 786440 | tf_op jit(solution)/shard_map/ppermute | solution.py:82
  94.6 24.2 %collective-permute-start.25 = (bf16[128,1024]{1,0:T(8,128)(2,1)}, bf16[128,1024]{1,0:T(8,128)(2,1)S(1)}, u32[]{:S(2)}, u32[]{:S(2)}) collective-permute-start(bf16[128,1024]{1,0:T(8,128)(2,1)} %collective-permute-done.24), channel_id=1, source_target_pairs={{0,62},{1,63},{2,0},{3,1},{4,2},{5,3},{6,4},{7,5},{8,6},{9,7},{10,... | collective-permute-start | bytes 786440 | tf_op jit(solution)/shard_map/ppermute | solution.py:82
  98.9 23.2 %collective-permute-start.17 = (bf16[128,1024]{1,0:T(8,128)(2,1)S(1)}, bf16[128,1024]{1,0:T(8,128)(2,1)S(1)}, u32[]{:S(2)}, u32[]{:S(2)}) collective-permute-start(bf16[128,1024]{1,0:T(8,128)(2,1)S(1)} %collective-permute-done.16), channel_id=1, source_target_pairs={{0,62},{1,63},{2,0},{3,1},{4,2},{5,3},{6,4},{7,5},{8,6},{9,7},{10,... | collective-permute-start | bytes 786440 | tf_op jit(solution)/shard_map/ppermute | solution.py:82
  107.2 22.5 %collective-permute-start.5 = (bf16[128,1024]{1,0:T(8,128)(2,1)S(1)}, bf16[128,1024]{1,0:T(8,128)(2,1)S(1)}, u32[]{:S(2)}, u32[]{:S(2)}) collective-permute-start(bf16[128,1024]{1,0:T(8,128)(2,1)S(1)} %collective-permute-done.3), channel_id=1, source_target_pairs={{0,2},{1,3},{2,4},{3,5},{4,6},{5,7},{6,8},{7,9},{8,10},{9,11},{10,... | collective-permute-start | bytes 786440 | tf_op jit(solution)/shard_map/ppermute | solution.py:82
  118.6 22.3 %collective-permute-start.4 = (bf16[128,1024]{1,0:T(8,128)(2,1)S(1)}, bf16[128,1024]{1,0:T(8,128)(2,1)S(1)}, u32[]{:S(2)}, u32[]{:S(2)}) collective-permute-start(bf16[128,1024]{1,0:T(8,128)(2,1)S(1)} %collective-permute-done.2), channel_id=1, source_target_pairs={{0,2},{1,3},{2,4},{3,5},{4,6},{5,7},{6,8},{7,9},{8,10},{9,11},{10,... | collective-permute-start | bytes 786440 | tf_op jit(solution)/shard_map/ppermute | solution.py:82
  118.8 22.2 %collective-permute-start.26 = (bf16[128,1024]{1,0:T(8,128)(2,1)S(1)}, bf16[128,1024]{1,0:T(8,128)(2,1)S(1)}, u32[]{:S(2)}, u32[]{:S(2)}) collective-permute-start(bf16[128,1024]{1,0:T(8,128)(2,1)S(1)} %collective-permute-done.25), channel_id=1, source_target_pairs={{0,62},{1,63},{2,0},{3,1},{4,2},{5,3},{6,4},{7,5},{8,6},{9,7},{10,... | collective-permute-start | bytes 786440 | tf_op jit(solution)/shard_map/ppermute | solution.py:82
  122.1 22.3 %collective-permute-start.18 = (bf16[128,1024]{1,0:T(8,128)(2,1)S(1)}, bf16[128,1024]{1,0:T(8,128)(2,1)S(1)}, u32[]{:S(2)}, u32[]{:S(2)}) collective-permute-start(bf16[128,1024]{1,0:T(8,128)(2,1)S(1)} %collective-permute-done.17), channel_id=1, source_target_pairs={{0,62},{1,63},{2,0},{3,1},{4,2},{5,3},{6,4},{7,5},{8,6},{9,7},{10,... | collective-permute-start | bytes 786440 | tf_op jit(solution)/shard_map/ppermute | solution.py:82
  129.7 22.5 %collective-permute-start.7 = (bf16[128,1024]{1,0:T(8,128)(2,1)S(1)}, bf16[128,1024]{1,0:T(8,128)(2,1)S(1)}, u32[]{:S(2)}, u32[]{:S(2)}) collective-permute-start(bf16[128,1024]{1,0:T(8,128)(2,1)S(1)} %collective-permute-done.5), channel_id=1, source_target_pairs={{0,2},{1,3},{2,4},{3,5},{4,6},{5,7},{6,8},{7,9},{8,10},{9,11},{10,... | collective-permute-start | bytes 786440 | tf_op jit(solution)/shard_map/ppermute | solution.py:82
  140.9 22.5 %collective-permute-start.6 = (bf16[128,1024]{1,0:T(8,128)(2,1)S(1)}, bf16[128,1024]{1,0:T(8,128)(2,1)S(1)}, u32[]{:S(2)}, u32[]{:S(2)}) collective-permute-start(bf16[128,1024]{1,0:T(8,128)(2,1)S(1)} %collective-permute-done.4), channel_id=1, source_target_pairs={{0,2},{1,3},{2,4},{3,5},{4,6},{5,7},{6,8},{7,9},{8,10},{9,11},{10,... | collective-permute-start | bytes 786440 | tf_op jit(solution)/shard_map/ppermute | solution.py:82
  140.9 22.5 %collective-permute-start.27 = (bf16[128,1024]{1,0:T(8,128)(2,1)S(1)}, bf16[128,1024]{1,0:T(8,128)(2,1)S(1)}, u32[]{:S(2)}, u32[]{:S(2)}) collective-permute-start(bf16[128,1024]{1,0:T(8,128)(2,1)S(1)} %collective-permute-done.26), channel_id=1, source_target_pairs={{0,62},{1,63},{2,0},{3,1},{4,2},{5,3},{6,4},{7,5},{8,6},{9,7},{10,... | collective-permute-start | bytes 786440 | tf_op jit(solution)/shard_map/ppermute | solution.py:82
  144.5 22.2 %collective-permute-start.19 = (bf16[128,1024]{1,0:T(8,128)(2,1)S(1)}, bf16[128,1024]{1,0:T(8,128)(2,1)S(1)}, u32[]{:S(2)}, u32[]{:S(2)}) collective-permute-start(bf16[128,1024]{1,0:T(8,128)(2,1)S(1)} %collective-permute-done.18), channel_id=1, source_target_pairs={{0,62},{1,63},{2,0},{3,1},{4,2},{5,3},{6,4},{7,5},{8,6},{9,7},{10,... | collective-permute-start | bytes 786440 | tf_op jit(solution)/shard_map/ppermute | solution.py:82
  152.2 22.5 %collective-permute-start.9 = (bf16[128,1024]{1,0:T(8,128)(2,1)S(1)}, bf16[128,1024]{1,0:T(8,128)(2,1)S(1)}, u32[]{:S(2)}, u32[]{:S(2)}) collective-permute-start(bf16[128,1024]{1,0:T(8,128)(2,1)S(1)} %collective-permute-done.7), channel_id=1, source_target_pairs={{0,2},{1,3},{2,4},{3,5},{4,6},{5,7},{6,8},{7,9},{8,10},{9,11},{10,... | collective-permute-start | bytes 786440 | tf_op jit(solution)/shard_map/ppermute | solution.py:82
  163.4 22.5 %collective-permute-start.8 = (bf16[128,1024]{1,0:T(8,128)(2,1)S(1)}, bf16[128,1024]{1,0:T(8,128)(2,1)S(1)}, u32[]{:S(2)}, u32[]{:S(2)}) collective-permute-start(bf16[128,1024]{1,0:T(8,128)(2,1)S(1)} %collective-permute-done.6), channel_id=1, source_target_pairs={{0,2},{1,3},{2,4},{3,5},{4,6},{5,7},{6,8},{7,9},{8,10},{9,11},{10,... | collective-permute-start | bytes 786440 | tf_op jit(solution)/shard_map/ppermute | solution.py:82
  163.4 22.5 %collective-permute-start.28 = (bf16[128,1024]{1,0:T(8,128)(2,1)S(1)}, bf16[128,1024]{1,0:T(8,128)(2,1)S(1)}, u32[]{:S(2)}, u32[]{:S(2)}) collective-permute-start(bf16[128,1024]{1,0:T(8,128)(2,1)S(1)} %collective-permute-done.27), channel_id=1, source_target_pairs={{0,62},{1,63},{2,0},{3,1},{4,2},{5,3},{6,4},{7,5},{8,6},{9,7},{10,... | collective-permute-start | bytes 786440 | tf_op jit(solution)/shard_map/ppermute | solution.py:82
  166.6 31.1 %collective-permute-start.20 = (bf16[128,1024]{1,0:T(8,128)(2,1)S(1)}, bf16[128,1024]{1,0:T(8,128)(2,1)S(1)}, u32[]{:S(2)}, u32[]{:S(2)}) collective-permute-start(bf16[128,1024]{1,0:T(8,128)(2,1)S(1)} %collective-permute-done.19), channel_id=1, source_target_pairs={{0,62},{1,63},{2,0},{3,1},{4,2},{5,3},{6,4},{7,5},{8,6},{9,7},{10,... | collective-permute-start | bytes 786440 | tf_op jit(solution)/shard_map/ppermute | solution.py:82
  174.6 23.9 %collective-permute-start.11 = (bf16[128,1024]{1,0:T(8,128)(2,1)S(1)}, bf16[128,1024]{1,0:T(8,128)(2,1)S(1)}, u32[]{:S(2)}, u32[]{:S(2)}) collective-permute-start(bf16[128,1024]{1,0:T(8,128)(2,1)S(1)} %collective-permute-done.9), channel_id=1, source_target_pairs={{0,2},{1,3},{2,4},{3,5},{4,6},{5,7},{6,8},{7,9},{8,10},{9,11},{10,... | collective-permute-start | bytes 786440 | tf_op jit(solution)/shard_map/ppermute | solution.py:82
  185.9 22.5 %collective-permute-start.10 = (bf16[128,1024]{1,0:T(8,128)(2,1)S(1)}, bf16[128,1024]{1,0:T(8,128)(2,1)S(1)}, u32[]{:S(2)}, u32[]{:S(2)}) collective-permute-start(bf16[128,1024]{1,0:T(8,128)(2,1)S(1)} %collective-permute-done.8), channel_id=1, source_target_pairs={{0,2},{1,3},{2,4},{3,5},{4,6},{5,7},{6,8},{7,9},{8,10},{9,11},{10,... | collective-permute-start | bytes 786440 | tf_op jit(solution)/shard_map/ppermute | solution.py:82
  185.9 24.0 %collective-permute-start.29 = (bf16[128,1024]{1,0:T(8,128)(2,1)S(1)}, bf16[128,1024]{1,0:T(8,128)(2,1)S(1)}, u32[]{:S(2)}, u32[]{:S(2)}) collective-permute-start(bf16[128,1024]{1,0:T(8,128)(2,1)S(1)} %collective-permute-done.28), channel_id=1, source_target_pairs={{0,62},{1,63},{2,0},{3,1},{4,2},{5,3},{6,4},{7,5},{8,6},{9,7},{10,... | collective-permute-start | bytes 786440 | tf_op jit(solution)/shard_map/ppermute | solution.py:82
  197.8 19.9 %collective-permute-start.21 = (bf16[128,1024]{1,0:T(8,128)(2,1)S(1)}, bf16[128,1024]{1,0:T(8,128)(2,1)S(1)}, u32[]{:S(2)}, u32[]{:S(2)}) collective-permute-start(bf16[128,1024]{1,0:T(8,128)(2,1)S(1)} %collective-permute-done.20), channel_id=1, source_target_pairs={{0,62},{1,63},{2,0},{3,1},{4,2},{5,3},{6,4},{7,5},{8,6},{9,7},{10,... | collective-permute-start | bytes 786440 | tf_op jit(solution)/shard_map/ppermute | solution.py:82
  198.5 23.4 %collective-permute-start.13 = (bf16[128,1024]{1,0:T(8,128)(2,1)S(1)}, bf16[128,1024]{1,0:T(8,128)(2,1)S(1)}, u32[]{:S(2)}, u32[]{:S(2)}) collective-permute-start(bf16[128,1024]{1,0:T(8,128)(2,1)S(1)} %collective-permute-done.11), channel_id=1, source_target_pairs={{0,2},{1,3},{2,4},{3,5},{4,6},{5,7},{6,8},{7,9},{8,10},{9,11},{10,... | collective-permute-start | bytes 786440 | tf_op jit(solution)/shard_map/ppermute | solution.py:82
  208.3 15.8 %collective-permute-start.12 = (bf16[128,1024]{1,0:T(8,128)(2,1)S(1)}, bf16[128,1024]{1,0:T(8,128)(2,1)S(1)}, u32[]{:S(2)}, u32[]{:S(2)}) collective-permute-start(bf16[128,1024]{1,0:T(8,128)(2,1)S(1)} %collective-permute-done.10), channel_id=1, source_target_pairs={{0,2},{1,3},{2,4},{3,5},{4,6},{5,7},{6,8},{7,9},{8,10},{9,11},{10,... | collective-permute-start | bytes 786440 | tf_op jit(solution)/shard_map/ppermute | solution.py:82
  209.9 14.3 %collective-permute-start.30 = (bf16[128,1024]{1,0:T(8,128)(2,1)S(1)}, bf16[128,1024]{1,0:T(8,128)(2,1)S(1)}, u32[]{:S(2)}, u32[]{:S(2)}) collective-permute-start(bf16[128,1024]{1,0:T(8,128)(2,1)S(1)} %collective-permute-done.29), channel_id=1, source_target_pairs={{0,62},{1,63},{2,0},{3,1},{4,2},{5,3},{6,4},{7,5},{8,6},{9,7},{10,... | collective-permute-start | bytes 786440 | tf_op jit(solution)/shard_map/ppermute | solution.py:82
  224.2 13.4 %collective-permute-start.31 = (bf16[128,1024]{1,0:T(8,128)(2,1)S(1)}, bf16[128,1024]{1,0:T(8,128)(2,1)S(1)}, u32[]{:S(2)}, u32[]{:S(2)}) collective-permute-start(bf16[128,1024]{1,0:T(8,128)(2,1)S(1)} %collective-permute-done.30), channel_id=1, source_target_pairs={{0,62},{1,63},{2,0},{3,1},{4,2},{5,3},{6,4},{7,5},{8,6},{9,7},{10,... | collective-permute-start | bytes 786440 | tf_op jit(solution)/shard_map/ppermute | solution.py:82
  244.4 18.7 %collective-permute-start.32 = (bf16[17,8,2048]{2,1,0:T(8,128)(2,1)S(1)}, bf16[17,8,2048]{2,1,0:T(8,128)(2,1)S(1)}, u32[]{:S(2)}, u32[]{:S(2)}) collective-permute-start(bf16[17,8,2048]{2,1,0:T(8,128)(2,1)S(1)} %get-tuple-element.27), channel_id=1, source_target_pairs={{0,1},{1,0},{2,3},{3,2},{4,5},{5,4},{6,7},{7,6},{8,9},{9,8},{10,11... | collective-permute-start | bytes 1671176 | tf_op jit(solution)/shard_map/ppermute | solution.py:85
  245.1 13.7 %collective-permute-start.36 = (bf16[104,1024]{1,0:T(8,128)(2,1)S(1)}, bf16[104,1024]{1,0:T(8,128)(2,1)S(1)}, u32[]{:S(2)}, u32[]{:S(2)}) collective-permute-start(bf16[104,1024]{1,0:T(8,128)(2,1)S(1)} %slice.1313), channel_id=1, source_target_pairs={{0,2},{1,3},{2,4},{3,5},{4,6},{5,7},{6,8},{7,9},{8,10},{9,11},{10,... | collective-permute-start | bytes 638984 | tf_op jit(solution)/shard_map/ppermute | solution.py:82
  (130 other events, 1459.3 us)
Sparse Core Ops, SparseCore 0:
  9.9 211.7 all-gather.1
